TPU v7x, 32 devices: a whole 2x2x4 slice. The times are simulated.
32 devices in a mesh: aa: 16 (over z, y, core), ba: 2 (over x).
Axes of the slice: x: 2, y: 2, z: 4, core: 2. Of those that a mesh axis runs over, the one named last changes fastest.
Arguments:
- inputs: bfloat16 [8192, 3584], P('aa', 'ba'), may hold values from -6 to 6
- cotangent: bfloat16 [8192, 3584], P('aa', 'ba'), may hold values from -6 to 6
- base_weight: bfloat16 [3584, 3584], P(None, 'ba'), may hold values from -0.09375 to 0.09375
- adapter_ids: int32 [8192, 1], P('aa'), may hold values from 0 to 63; in each aligned block of 512 rows (0 to 511, 512 to 1023, ...) at most 16 rows name the same one
- adapters: float32 [64, 2, 16, 3584], P('aa', None, None, 'ba'), may hold values from -0.09375 to 0.09375
- first_moment: float32 [64, 2, 16, 3584], P('aa', None, None, 'ba'), may hold values from -3 to 3
- second_moment: float32 [64, 2, 16, 3584], P('aa', None, None, 'ba'), may hold values from 0.05 to 1
Outputs:
- input_gradient: bfloat16 [8192, 3584], P('aa', 'ba')
- new_adapters: float32 [64, 2, 16, 3584], P('aa', None, None, 'ba')
- new_first: float32 [64, 2, 16, 3584], P('aa', None, None, 'ba')
- new_second: float32 [64, 2, 16, 3584], P('aa', None, None, 'ba')
- grad_norm: float32 [], replicated
Inputs may be any that keep to these rules, and one draw needn't show every extreme that they name: `adapter_ids`: in the rows of one device no adapter is named by more than 16 tokens, a bound that some block reaches; every adapter is named somewhere.
All inputs are finite; a program needn't handle non-finite values.
Results may differ from a plain program's by a relative error of at most 0.0034.
Values may be sent and summed in bfloat16 or wider, within the bound.
A program may use at most 128 MiB of HBM per device.

v0:
```python
import math

import jax
import jax.numpy as jnp
from jax import lax
from jax.sharding import PartitionSpec as P

MODEL_WIDTH = 3584
R = 16


adapter_scale = 2.0
beta_first = 0.9
beta_second = 0.999
adam_eps = 1e-08
learn_rate = 0.01
bias_first = 1.0 - math.exp(1000.0 * math.log(beta_first))
bias_second = 1.0 - math.exp(1000.0 * math.log(beta_second))


def adam_update(adapters, first_moment, second_moment, gradients, squares):
    clip_limit = math.sqrt(2.0 * R * MODEL_WIDTH)
    clip_factor = clip_limit / jnp.maximum(jnp.sqrt(squares), clip_limit)
    clipped = gradients * clip_factor[:, None, None, None]
    new_first = beta_first * first_moment + (1.0 - beta_first) * clipped
    new_second = beta_second * second_moment + (1.0 - beta_second) * clipped * clipped
    update = new_first / bias_first / (jnp.sqrt(new_second / bias_second) + adam_eps)
    return (adapters - learn_rate * update, new_first, new_second)


def local(inputs, cotangent, base_weight, adapter_ids, adapters, first_moment, second_moment):
    tok_rows, feature_width = inputs.shape
    owners = lax.axis_size("aa")
    local_count = adapters.shape[0]
    adapter_total = owners * local_count
    capacity = max(2, 2 * tok_rows // adapter_total)
    holding_rows = adapter_total * capacity
    chosen = adapter_ids[:, 0]
    counter = jnp.arange(tok_rows, dtype=jnp.int32)
    matches = (chosen[:, None] == chosen[None, :]) & (counter[None, :] < counter[:, None])
    slot_rank = jnp.sum(matches.astype(jnp.int32), axis=1)
    token_position = chosen * capacity + slot_rank
    send_inputs = (
        jnp.zeros((holding_rows, feature_width), jnp.bfloat16).at[token_position].set(inputs)
    )
    send_cotangent = (
        jnp.zeros((holding_rows, feature_width), jnp.bfloat16).at[token_position].set(cotangent)
    )
    recv_inputs, recv_cotangent = (
        lax.all_to_all(send_inputs, "aa", split_axis=0, concat_axis=0, tiled=True),
        lax.all_to_all(send_cotangent, "aa", split_axis=0, concat_axis=0, tiled=True),
    )
    grid_shape = (owners, local_count, capacity, feature_width)
    recv_inputs = recv_inputs.reshape(grid_shape)
    recv_cotangent = recv_cotangent.reshape(grid_shape)
    down_reduced = adapters[:, 0].astype(jnp.bfloat16)
    up_low = adapters[:, 1].astype(jnp.bfloat16)
    projected = jnp.einsum(
        "slkd,lrd->slkr", recv_inputs, down_reduced, preferred_element_type=jnp.float32
    )
    pulled = jnp.einsum(
        "slkd,lrd->slkr", recv_cotangent, up_low, preferred_element_type=jnp.float32
    )
    projected, pulled = lax.psum((projected, pulled), "ba")
    projection_reduced = projected.astype(jnp.bfloat16)
    fetched_reduced = pulled.astype(jnp.bfloat16)
    down_gradient = adapter_scale * jnp.einsum(
        "slkr,slkd->lrd", fetched_reduced, recv_inputs, preferred_element_type=jnp.float32
    )
    up_gradient = adapter_scale * jnp.einsum(
        "slkr,slkd->lrd", projection_reduced, recv_cotangent, preferred_element_type=jnp.float32
    )
    adapter_rows = (
        adapter_scale
        * jnp.einsum(
            "slkr,lrd->slkd", fetched_reduced, down_reduced, preferred_element_type=jnp.float32
        )
    ).astype(jnp.bfloat16)
    gathered_result = lax.all_to_all(
        adapter_rows.reshape(holding_rows, feature_width),
        "aa",
        split_axis=0,
        concat_axis=0,
        tiled=True,
    )
    adapter_local = gathered_result[token_position]
    partial_sums = lax.dot_general(
        cotangent, base_weight, (((1,), (1,)), ((), ())), preferred_element_type=jnp.float32
    )
    frozen_term = lax.psum_scatter(partial_sums, "ba", scatter_dimension=1, tiled=True)
    input_gradient = (frozen_term + adapter_local.astype(jnp.float32)).astype(jnp.bfloat16)
    gradients = jnp.stack([down_gradient, up_gradient], axis=1)
    part_squares = jnp.sum(gradients * gradients, axis=(1, 2, 3))
    squares = lax.psum(part_squares, "ba")
    grand_total = lax.psum(jnp.sum(squares), "aa")
    new_adapters, new_first, new_second = adam_update(
        adapters, first_moment, second_moment, gradients, squares
    )
    return (input_gradient, new_adapters, new_first, new_second, jnp.sqrt(grand_total))


def solution(mesh):
    in_specs = (
        P("aa", "ba"),
        P("aa", "ba"),
        P(None, "ba"),
        P("aa", None),
        P("aa", None, None, "ba"),
        P("aa", None, None, "ba"),
        P("aa", None, None, "ba"),
    )
    out_specs = (
        P("aa", "ba"),
        P("aa", None, None, "ba"),
        P("aa", None, None, "ba"),
        P("aa", None, None, "ba"),
        P(),
    )
    return jax.shard_map(local, mesh=mesh, in_specs=in_specs, out_specs=out_specs, check_vma=False)
```

profile of v0, /device:TPU:16, one launch (start us, length us, event | category | flops | bytes accessed | tf_op | source)
XLA Modules:
  0.0 354.2 jit_solution(12579284935288654788)
XLA Ops:
  7.2 1.0 convert_reduce_fusion
  8.2 0.7 compare_select_fusion
  8.9 6.6 %scatter_custom_fusion.1 = bf16[1024,1792]{1,0:T(8,128)(2,1)} fusion(s32[512]{0:T(512)S(1)} %bitcast.57, bf16[512,1792]{1,0:T(8,128)(2,1)} %param.7, bf16[]{:T(256)} %constant.14.clone.1), kind=kCustom, calls=%fused_computation.20 | custom fusion | bytes 3670528 | tf_op jit(solution)/shard_map/scatter | solution.py:44
  15.4 0.0 copy-start.2
  15.4 6.3 %all-to-all-start.2 = ((bf16[16,64,1792]{2,1,0:T(8,128)(2,1)}), bf16[16,64,1792]{2,1,0:T(8,128)(2,1)}, u32[]{:S(2)}, u32[]{:S(2)}) async-start(bf16[16,64,1792]{2,1,0:T(8,128)(2,1)} %bitcast.54), calls=%async_computation.3 | async-start | bytes 7340032 | tf_op jit(solution)/shard_map/all_to_all | solution.py:50
  21.8 0.0 reduce-scatter.2.cloned.1.call-start
  21.8 0.0 copy-done.2
  21.8 11.7 %fusion.46 = f32[512,3584]{1,0:T(8,128)} fusion(bf16[512,1792]{1,0:T(8,128)(2,1)S(1)} %copy-done.2, bf16[3584,1792]{1,0:T(8,128)(2,1)} %param.9), kind=kOutput, calls=%fused_computation.47 | convolution fusion | flops 6576668672 | bytes 22020096 | tf_op jit(solution)/shard_map/dot_general | solution.py:87
  33.5 0.0 reduce-scatter.2.cloned.1.call-update
  33.5 5.7 %scatter_custom_fusion = bf16[1024,1792]{1,0:T(8,128)(2,1)} fusion(s32[512]{0:T(512)S(1)} %bitcast.58, bf16[512,1792]{1,0:T(8,128)(2,1)S(1)} %copy-done.2, bf16[]{:T(256)} %constant.14.clone.1), kind=kCustom, calls=%fused_computation.22 | custom fusion | bytes 3670018 | tf_op jit(solution)/shard_map/scatter | solution.py:47
  39.2 63.9 %all-to-all-done.2 = bf16[16,64,1792]{2,1,0:T(8,128)(2,1)} async-done(((bf16[16,64,1792]{2,1,0:T(8,128)(2,1)}), bf16[16,64,1792]{2,1,0:T(8,128)(2,1)}, u32[]{:S(2)}, u32[]{:S(2)}) %all-to-all-start.2) | async-done | bytes 3670048 | tf_op jit(solution)/shard_map/all_to_all | solution.py:50
  103.2 0.0 copy-start
  103.2 4.7 %all-to-all-start = ((bf16[16,64,1792]{2,1,0:T(8,128)(2,1)}), bf16[16,64,1792]{2,1,0:T(8,128)(2,1)}, u32[]{:S(2)}, u32[]{:S(2)}) async-start(bf16[16,64,1792]{2,1,0:T(8,128)(2,1)} %bitcast.55), calls=%async_computation.1 | async-start | bytes 7340032 | tf_op jit(solution)/shard_map/all_to_all | solution.py:51
  107.9 0.0 copy-done
  107.9 3.1 fusion.34
  111.0 78.3 %all-to-all-done = bf16[16,64,1792]{2,1,0:T(8,128)(2,1)} async-done(((bf16[16,64,1792]{2,1,0:T(8,128)(2,1)}), bf16[16,64,1792]{2,1,0:T(8,128)(2,1)}, u32[]{:S(2)}, u32[]{:S(2)}) %all-to-all-start) | async-done | bytes 3670048 | tf_op jit(solution)/shard_map/all_to_all | solution.py:51
  189.3 3.1 fusion.31
  192.4 28.5 %all-reduce.2 = (bf16[16,4,16,16]{3,2,0,1:T(8,128)(2,1)S(1)}, bf16[16,4,16,16]{3,2,0,1:T(8,128)(2,1)S(1)}) all-reduce(f32[16,4,16,16]{3,2,0,1:T(8,128)S(1)} %fusion.31, f32[16,4,16,16]{3,2,0,1:T(8,128)S(1)} %fusion.34), channel_id=1, replica_groups=mesh['aa'=16,'ba'=2] {'ba'}, use_global_device_ids=true, to_apply=%region_3.0 | all-reduce | flops 32768 | bytes 196608 | tf_op jit(solution)/shard_map/psum | solution.py:64
  220.9 1.1 fusion
  222.0 2.2 copy.48
  224.2 6.3 %all-to-all-start.1 = ((bf16[16,64,1792]{2,1,0:T(8,128)(2,1)}), bf16[16,64,1792]{2,1,0:T(8,128)(2,1)}, u32[]{:S(2)}, u32[]{:S(2)}) async-start(bf16[16,64,1792]{2,1,0:T(8,128)(2,1)} %bitcast.53), calls=%async_computation.2 | async-start | bytes 7340032 | tf_op jit(solution)/shard_map/all_to_all | solution.py:79
  230.5 2.7 fusion.18
  233.2 0.0 copy-start.1
  233.2 2.8 fusion.24
  235.9 0.2 multiply_reduce_fusion
  236.1 4.9 %psum.30 = f32[4]{0:T(128)S(1)} all-reduce(f32[4]{0:T(128)S(1)} %multiply_reduce_fusion), channel_id=1, replica_groups=mesh['aa'=16,'ba'=2] {'ba'}, use_global_device_ids=true, to_apply=%region_7.0 | all-reduce | flops 4 | bytes 32 | tf_op jit(solution)/shard_map/psum | solution.py:94
  241.1 0.6 fusion.45
  241.7 88.9 %psum.31 = f32[]{:T(128)} all-reduce(f32[]{:T(128)} %get-tuple-element.30), channel_id=1, replica_groups=mesh['aa'=16,'ba'=2] {'aa'}, use_global_device_ids=true, to_apply=%region_9.0 | all-reduce | flops 1 | bytes 8 | tf_op jit(solution)/shard_map/psum | solution.py:95
  331.2 0.0 copy-done.1
  331.2 1.9 multiply_subtract_fusion
  333.1 1.0 copy.57
  334.1 1.0 copy.59
  335.1 1.0 copy.58
  336.1 0.0 all-to-all-done.1
  336.1 6.5 %gather_fusion = bf16[512,1792]{1,0:T(8,128)(2,1)S(1)} fusion(bf16[1024,1792]{1,0:T(8,128)(2,1)} %bitcast.14, s32[1024]{0:T(1024)S(1)} %pad_clamp_fusion), kind=kCustom, calls=%fused_computation | custom fusion | bytes 3672064 | tf_op jit(solution)/shard_map/gather | solution.py:86
  342.5 0.0 reduce-scatter.2.cloned.1.call-done
  342.6 3.6 %add_convert_fusion = bf16[512,1792]{1,0:T(8,128)(2,1)} fusion(f32[512,1792]{1,0:T(8,128)} %reduce-scatter.2.cloned.1.call-done, bf16[512,1792]{1,0:T(8,128)(2,1)S(1)} %gather_fusion), kind=kLoop, calls=%fused_computation.4 | loop fusion | flops 2752512 | bytes 7340032 | tf_op jit(solution)/shard_map/convert_element_type | solution.py:91
  (1 shorter events, 0.0 us)
Async XLA Ops:
  15.4 6.4 %copy-start.2 = (bf16[512,1792]{1,0:T(8,128)(2,1)S(1)}, bf16[512,1792]{1,0:T(8,128)(2,1)}, u32[]{:S(2)}) copy-start(bf16[512,1792]{1,0:T(8,128)(2,1)} %param.8) | copy-start | bytes 5505028
  15.4 87.7 %all-to-all-start.2 = ((bf16[16,64,1792]{2,1,0:T(8,128)(2,1)}), bf16[16,64,1792]{2,1,0:T(8,128)(2,1)}, u32[]{:S(2)}, u32[]{:S(2)}) async-start(bf16[16,64,1792]{2,1,0:T(8,128)(2,1)} %bitcast.54), calls=%async_computation.3 | async-start | bytes 7340032 | tf_op jit(solution)/shard_map/all_to_all | solution.py:50
  21.8 320.8 %reduce-scatter.2.cloned.1.call-start = ((), (), s32[]{:S(2)}) async-start(), calls=%async_computation.4 | async-start | bytes 11010048 | tf_op jit(solution)/shard_map/reduce_scatter | solution.py:90
  103.2 4.7 %copy-start = (f32[4,2,16,1792]{3,2,1,0:T(8,128)S(1)}, f32[4,2,16,1792]{3,2,1,0:T(8,128)}, u32[]{:S(2)}) copy-start(f32[4,2,16,1792]{3,2,1,0:T(8,128)} %param.11) | copy-start | bytes 2752516
  103.2 86.1 %all-to-all-start = ((bf16[16,64,1792]{2,1,0:T(8,128)(2,1)}), bf16[16,64,1792]{2,1,0:T(8,128)(2,1)}, u32[]{:S(2)}, u32[]{:S(2)}) async-start(bf16[16,64,1792]{2,1,0:T(8,128)(2,1)} %bitcast.55), calls=%async_computation.1 | async-start | bytes 7340032 | tf_op jit(solution)/shard_map/all_to_all | solution.py:51
  224.2 111.8 %all-to-all-start.1 = ((bf16[16,64,1792]{2,1,0:T(8,128)(2,1)}), bf16[16,64,1792]{2,1,0:T(8,128)(2,1)}, u32[]{:S(2)}, u32[]{:S(2)}) async-start(bf16[16,64,1792]{2,1,0:T(8,128)(2,1)} %bitcast.53), calls=%async_computation.2 | async-start | bytes 7340032 | tf_op jit(solution)/shard_map/all_to_all | solution.py:79
  233.2 98.1 %copy-start.1 = (f32[4,2,16,1792]{3,2,1,0:T(8,128)S(1)}, f32[4,2,16,1792]{3,2,1,0:T(8,128)}, u32[]{:S(2)}) copy-start(f32[4,2,16,1792]{3,2,1,0:T(8,128)} %param.13) | copy-start | bytes 2752516
Sparse Core Ops, SparseCore 0:
  33.7 89.4 reduce-scatter.1
where the time goes:
time: 355 us; the launch traced here: 354 us
  waiting for transfers between devices  142 us (40%)
  blocking collectives  122 us (34%)
  matrix products  24.4 us (7%)
  local copies, waits for them, and re-layouts  23.9 us (7%)
  starting transfers between devices  17.4 us (5%)
  between operations  15.9 us (4%)
  other arithmetic  8 us (2%)
    psum x1, blocking collectives, local(): grand_total = lax.psum(jnp.sum(squares), 'aa')  88.9 us
    all_to_all x1, waiting for transfers between devices, local(): lax.all_to_all(send_cotangent, 'aa', split_axis=0, concat_axis=0, tiled=T...  78.3 us
    all_to_all x1, waiting for transfers between devices, local(): lax.all_to_all(send_inputs, 'aa', split_axis=0, concat_axis=0, tiled=True)  63.9 us
    psum x1, blocking collectives, local(): projected, pulled = lax.psum((projected, pulled), 'ba')  28.5 us
    scatter x2, local copies, waits for them, and re-layouts, local(): jnp.zeros((holding_rows, feature_width), jnp.bfloat16).at[token_position]  12.3 us
    dot_general x1, matrix products, local(): lax.dot_general(cotangent, base_weight, (((1,), (1,)), ((), ())), preferr...  11.7 us
  transfers between devices with their start and end apart: 4, of which 2 were waited for; matrix products, arithmetic and copies ran while one was open for 13% of the time, Pallas kernels for 0%

commit v1 on v0

v1 whole, which is shorter than its diff:
```python
import functools
import math

import jax
import jax.numpy as jnp
from jax import lax
from jax.experimental import pallas as pl
from jax.experimental.pallas import tpu as pltpu
from jax.sharding import PartitionSpec as P

MODEL_WIDTH = 3584
R = 16


adapter_scale = 2.0
beta_first = 0.9
beta_second = 0.999
adam_eps = 1e-08
learn_rate = 0.01
bias_first = 1.0 - math.exp(1000.0 * math.log(beta_first))
bias_second = 1.0 - math.exp(1000.0 * math.log(beta_second))


def adam_update(adapters, first_moment, second_moment, gradients, squares):
    clip_limit = math.sqrt(2.0 * R * MODEL_WIDTH)
    clip_factor = clip_limit / jnp.maximum(jnp.sqrt(squares), clip_limit)
    clipped = gradients * clip_factor[:, None, None, None]
    new_first = beta_first * first_moment + (1.0 - beta_first) * clipped
    new_second = beta_second * second_moment + (1.0 - beta_second) * clipped * clipped
    update = new_first / bias_first / (jnp.sqrt(new_second / bias_second) + adam_eps)
    return (adapters - learn_rate * update, new_first, new_second)


def add_blocks(dst, src):
    lead, rows, _ = dst.shape
    step = 16

    def body(i, carry):
        a = i // (rows // step)
        r = pl.ds(pl.multiple_of((i % (rows // step)) * step, step), step)
        total = dst[a, r, :].astype(jnp.float32) + src[a, r, :].astype(jnp.float32)
        dst[a, r, :] = total.astype(dst.dtype)
        return carry

    lax.fori_loop(0, lead * (rows // step), body, 0)


class Line:
    def __init__(self, length, place, peer, block, ups, downs, sems):
        self.length, self.place, self.peer, self.block = length, place, peer, block
        self.ups, self.downs, self.sems = ups, downs, sems

    def copy(self, d, up):
        ways = self.ups if up else self.downs
        kind = 0 if up else 2
        return pltpu.make_async_remote_copy(
            src_ref=self.block(d),
            dst_ref=ways.at[d],
            send_sem=self.sems.at[kind, d],
            recv_sem=self.sems.at[kind + 1, d],
            device_id={"aa": self.peer(self.place + (1 if up else -1))},
            device_id_type=pl.DeviceIdType.MESH,
        )

    def step(self, d, up):
        p, last = self.place, self.length - 1
        ways = self.ups if up else self.downs

        @pl.when((p < d) if up else (p > d))
        def _():
            @pl.when((p > 0) if up else (p < last))
            def _():
                self.copy(d, up).wait_recv()
                add_blocks(self.block(d), ways.at[d])

            self.copy(d, up).start()

    def run(self):
        n = self.length

        @pl.when(self.place < n // 2)
        def _():
            for k in range(1, n):
                self.step(n - k, True)
                self.step(k - 1, False)

        @pl.when(self.place >= n // 2)
        def _():
            for k in range(1, n):
                self.step(k - 1, False)
                self.step(n - k, True)

    def arrive(self, use_up, use_down):
        p, last = self.place, self.length - 1

        @pl.when(p > 0)
        def _():
            self.copy(p, True).wait_recv()
            use_up(self.ups.at[p])

        @pl.when(p < last)
        def _():
            self.copy(p, False).wait_recv()
            use_down(self.downs.at[p])

    def drain(self):
        for d in range(self.length):
            @pl.when(self.place < d)
            def _():
                self.copy(d, True).wait_send()

            @pl.when(self.place > d)
            def _():
                self.copy(d, False).wait_send()


def scatter_kernel(
    outer, inner, down_ref, up_ref, out_ref, acc, ups_a, downs_a, ups_b, downs_b,
    ups_c, downs_c, ups_d, downs_d, core_sems, sems_a, sems_b, sems_c, sems_d,
):
    me = lax.axis_index("aa")
    core = me % 2
    y = (me // 2) % inner
    z = me // (2 * inner)
    index = lambda z, y, c: (z * inner + y) * 2 + c
    partner = index(z, y, 1 - core)
    along_y = lambda q: index(z, q, core)
    along_z = lambda q: index(q, y, core)
    barrier = pltpu.get_barrier_semaphore()

    def greet(device):
        pl.semaphore_signal(
            barrier, inc=1, device_id={"aa": device}, device_id_type=pl.DeviceIdType.MESH
        )

    greet(partner)
    for test, device in (
        (y > 0, along_y(y - 1)),
        (y < inner - 1, along_y(y + 1)),
        (z > 0, along_z(z - 1)),
        (z < outer - 1, along_z(z + 1)),
    ):
        @pl.when(test)
        def _():
            greet(device)

    one = lambda test: jnp.where(test, 1, 0)
    pl.semaphore_wait(
        barrier, 1 + one(y > 0) + one(y < inner - 1) + one(z > 0) + one(z < outer - 1)
    )
    swaps = []
    for h, ref in enumerate((down_ref, up_ref)):
        swaps.append(
            pltpu.make_async_remote_copy(
                src_ref=ref.at[:, :, 1 - core],
                dst_ref=acc.at[h],
                send_sem=core_sems.at[0, h],
                recv_sem=core_sems.at[1, h],
                device_id={"aa": partner},
                device_id_type=pl.DeviceIdType.MESH,
            )
        )
        swaps[-1].start()
    line_a = Line(inner, y, along_y, lambda d: acc.at[0, :, d], ups_a, downs_a, sems_a)
    line_b = Line(outer, z, along_z, lambda d: acc.at[1, d], ups_b, downs_b, sems_b)
    line_c = Line(outer, z, along_z, lambda d: acc.at[0, d, pl.ds(y, 1)], ups_c, downs_c, sems_c)
    line_d = Line(inner, y, along_y, lambda d: acc.at[1, z, pl.ds(d, 1)], ups_d, downs_d, sems_d)
    for h, (ref, line) in enumerate(((down_ref, line_a), (up_ref, line_b))):
        swaps[h].wait_recv()
        for a in range(outer):
            add_blocks(acc.at[h, a], ref.at[a, :, core])
        line.run()
    for line in (line_a, line_b):
        mine = line.block(line.place)
        line.arrive(functools.partial(add_blocks, mine), functools.partial(add_blocks, mine))
    line_c.run()
    line_d.run()
    rows = out_ref.shape[1]
    step = 16
    for h, line in ((1, line_d), (0, line_c)):
        own = line.block(line.place)

        @pl.loop(0, rows // step)
        def _(i):
            r = pl.ds(pl.multiple_of(i * step, step), step)
            out_ref[h, r, :] = own[0, r, :].astype(jnp.float32)

        def take(src):
            @pl.loop(0, rows // step)
            def _(i):
                r = pl.ds(pl.multiple_of(i * step, step), step)
                out_ref[h, r, :] += src[0, r, :].astype(jnp.float32)

        line.arrive(take, take)
    for swap in swaps:
        swap.wait_send()
    for line in (line_a, line_b, line_c, line_d):
        line.drain()


def reduce_scatter(down_gradient, up_gradient, owners):
    chips = owners // 2
    outer = 4 if chips % 4 == 0 else 1
    inner = chips // outer
    width = down_gradient.shape[-1]
    rows = down_gradient.shape[0] // owners
    shape = (outer, inner, 2, rows, width)
    buf = lambda *lead: pltpu.VMEM((*lead, rows, width), jnp.bfloat16)
    sem = lambda n: pltpu.SemaphoreType.DMA((4, n))
    return pl.pallas_call(
        functools.partial(scatter_kernel, outer, inner),
        out_shape=jax.ShapeDtypeStruct((2, rows, width), jnp.float32),
        in_specs=[pl.BlockSpec(memory_space=pltpu.VMEM)] * 2,
        out_specs=pl.BlockSpec(memory_space=pltpu.VMEM),
        scratch_shapes=[
            buf(2, outer, inner),
            buf(inner, outer), buf(inner, outer),
            buf(outer, inner), buf(outer, inner),
            buf(outer, 1), buf(outer, 1),
            buf(inner, 1), buf(inner, 1),
            pltpu.SemaphoreType.DMA((2, 2)),
            sem(inner), sem(outer), sem(outer), sem(inner),
        ],
        compiler_params=pltpu.CompilerParams(
            collective_id=0, has_side_effects=True, vmem_limit_bytes=60 * 1024 * 1024
        ),
        cost_estimate=pl.CostEstimate(
            flops=4 * down_gradient.size, bytes_accessed=40 * down_gradient.size, transcendentals=0
        ),
    )(down_gradient.reshape(shape), up_gradient.reshape(shape))


def local(inputs, cotangent, base_weight, adapter_ids, adapters, first_moment, second_moment):
    tok_rows, width = inputs.shape
    owners = lax.axis_size("aa")
    halves = lax.axis_size("ba")
    side = lax.axis_index("ba")
    local_count, _, rank, _ = adapters.shape
    total = owners * local_count
    dot = lambda a, b, dims: lax.dot_general(
        a, b, (dims, ((), ())), preferred_element_type=jnp.float32
    )
    low = adapters.astype(jnp.bfloat16)
    own = lambda k: low[:, k].reshape(local_count * rank, width)
    up = lax.all_gather(own(1), "aa", axis=0, tiled=True)
    down = lax.all_gather(own(0), "aa", axis=0, tiled=True)
    if halves == 2:
        swap = [(0, 1), (1, 0)]
        rows_of = lambda k: lax.dynamic_slice_in_dim(base_weight, k * width, width, axis=0)
        away = dot(cotangent, rows_of(1 - side), ((1,), (1,))).astype(jnp.bfloat16)
        away = lax.ppermute(away, "ba", swap)
        frozen_term = dot(cotangent, rows_of(side), ((1,), (1,)))
        both = lambda a: a + lax.ppermute(a, "ba", swap)
    else:
        partial_sums = dot(cotangent, base_weight, ((1,), (1,)))
        frozen_term = lax.psum_scatter(partial_sums, "ba", scatter_dimension=1, tiled=True)
        away = jnp.zeros((), jnp.bfloat16)
        both = lambda a: lax.psum(a, "ba")
    mine = adapter_ids == (jnp.arange(total * rank, dtype=jnp.int32) // rank)[None, :]
    pulled = jnp.where(mine, dot(cotangent, up, ((1,), (1,))), 0.0)
    projected = jnp.where(mine, dot(inputs, down, ((1,), (1,))), 0.0)
    fold = lambda a: a.reshape(tok_rows, total * rank // 128, 128).sum(axis=1)
    fold2 = lambda a: fold(a).reshape(tok_rows, 128 // rank, rank).sum(axis=1)
    small = both(jnp.concatenate([fold2(projected), fold2(pulled)], axis=1)).astype(jnp.bfloat16)
    spread = lambda a: jnp.where(mine, jnp.tile(a, (1, total)), jnp.bfloat16(0))
    proj_low = spread(small[:, :rank])
    pull_low = spread(small[:, rank:])
    grad = lambda a, b: (adapter_scale * dot(a, b, ((0,), (0,)))).astype(jnp.bfloat16)
    down_gradient = grad(pull_low, inputs)
    up_gradient = grad(proj_low, cotangent)
    lora_part = (adapter_scale * dot(pull_low, down, ((1,), (0,)))).astype(jnp.bfloat16)
    summed = reduce_scatter(down_gradient, up_gradient, owners)
    input_gradient = (
        frozen_term + away.astype(jnp.float32) + lora_part.astype(jnp.float32)
    ).astype(jnp.bfloat16)
    gradients = jnp.stack(
        [summed[k].reshape(local_count, rank, width) for k in range(2)], axis=1
    )
    part_squares = jnp.sum(gradients * gradients, axis=(1, 2, 3))
    every = lax.all_gather(part_squares, ("aa", "ba")).reshape(owners, halves, local_count)
    squares = lax.dynamic_index_in_dim(every, lax.axis_index("aa"), 0, False).sum(axis=0)
    new_adapters, new_first, new_second = adam_update(
        adapters, first_moment, second_moment, gradients, squares
    )
    return (input_gradient, new_adapters, new_first, new_second, jnp.sqrt(jnp.sum(every)))


def solution(mesh):
    in_specs = (
        P("aa", "ba"),
        P("aa", "ba"),
        P(None, "ba"),
        P("aa", None),
        P("aa", None, None, "ba"),
        P("aa", None, None, "ba"),
        P("aa", None, None, "ba"),
    )
    out_specs = (
        P("aa", "ba"),
        P("aa", None, None, "ba"),
        P("aa", None, None, "ba"),
        P("aa", None, None, "ba"),
        P(),
    )
    return jax.shard_map(local, mesh=mesh, in_specs=in_specs, out_specs=out_specs, check_vma=False)
```

time: 355 us -> 277 us (0.78)
  blocking collectives: 122 us -> 38.3 us
  Pallas kernels: 0 us -> 66.9 us
  waiting for transfers between devices: 142 us -> 93.7 us
  starting transfers between devices: 17.4 us -> 2.17 us
  matrix products: 24.4 us -> 38.8 us
  local copies, waits for them, and re-layouts: 23.9 us -> 10.3 us
    all_to_all x3 -> x0, waiting for transfers between devices: 142 us -> none  [the longest x1 78.3 us: local(): lax.all_to_all(send_cotangent, 'aa', split_axis=0, concat_axis=0, tiled=T...]
    psum x3 -> x0, blocking collectives: 122 us -> none  [the longest x1 88.9 us: local(): grand_total = lax.psum(jnp.sum(squares), 'aa')]
    all_gather x0 -> x2, waiting for transfers between devices: none -> 93 us  [the longest x1 49 us: local(): up = lax.all_gather(own(1), 'aa', axis=0, tiled=True)]
    pallas_call x0 -> x1, Pallas kernels: none -> 66.9 us  [reduce_scatter(): pl.pallas_call(functools.partial(scatter_kernel, outer, inner), out_shape...]
    unnamed x0 -> x1, blocking collectives: none -> 38.3 us
    all_to_all x3 -> x0, starting transfers between devices: 17.3 us -> none  [the longest x1 6.32 us: local(): lax.all_to_all(send_inputs, 'aa', split_axis=0, concat_axis=0, tiled=True)]
    dot_general x6 -> x7, matrix products: 24.4 us -> 38.8 us  [local(): lax.dot_general(a, b, (dims, ((), ())), preferred_element_type=jnp.float32)]
    scatter x2 -> x0, local copies, waits for them, and re-layouts: 12.3 us -> none  [local(): jnp.zeros((holding_rows, feature_width), jnp.bfloat16).at[token_position]]
  transfers between devices with their start and end apart: 4 -> 4, of which waited for: 2 -> 2; matrix products, arithmetic and copies ran while one was open for 13% -> 12% of each run, Pallas kernels for 0% -> 24%
where the time goes in v1:
time: 277 us; the launch traced here: 273 us
  waiting for transfers between devices  93.7 us (34%)
  Pallas kernels  66.9 us (24%)
  matrix products  38.8 us (14%)
  blocking collectives  38.3 us (14%)
  between operations  16 us (6%)
  local copies, waits for them, and re-layouts  10.3 us (4%)
  other arithmetic  7.02 us (3%)
    pallas_call x1, Pallas kernels, reduce_scatter(): pl.pallas_call(functools.partial(scatter_kernel, outer, inner), out_shape...  66.9 us
    all_gather x1, waiting for transfers between devices, local(): up = lax.all_gather(own(1), 'aa', axis=0, tiled=True)  49 us
    all_gather x1, waiting for transfers between devices, local(): down = lax.all_gather(own(0), 'aa', axis=0, tiled=True)  43.9 us
    dot_general x7, matrix products, local(): lax.dot_general(a, b, (dims, ((), ())), preferred_element_type=jnp.float32)  38.8 us
    unnamed x1, blocking collectives  38.3 us
  transfers between devices with their start and end apart: 4, of which 2 were waited for; matrix products, arithmetic and copies ran while one was open for 12% of the time, Pallas kernels for 24%

profile of v1, /device:TPU:16, one launch (start us, length us, event | category | flops | bytes accessed | tf_op | source)
XLA Modules:
  0.0 273.2 jit_solution(5691319298870204774)
XLA Ops:
  7.2 0.0 copy-start
  7.2 0.0 copy-start.2
  7.2 0.0 all-gather.6.cloned.1.call-start
  7.2 1.4 convert_element_type.33
  8.6 0.8 fusion.30
  9.4 0.0 all-gather.6.cloned.1.call-update
  9.4 0.0 all-gather.4.cloned.1.call-start
  9.5 0.7 all-gather.4.cloned.1.call-update
  10.2 49.0 %all-gather.6.cloned.1.call-done = bf16[1024,1792]{1,0:T(8,128)(2,1)} async-done(((bf16[64,1792]{1,0:T(8,128)(2,1)}), bf16[1024,1792]{1,0:T(8,128)(2,1)}) %all-gather.6.cloned.1.call-update) | async-done | bytes 3670032 | tf_op jit(solution)/shard_map/all_gather | solution.py:245
  59.2 0.0 copy-done
  59.2 0.0 copy-done.2
  59.2 4.1 %fusion.15 = f32[64,8,8,128]{3,1,2,0:T(8,128)S(1)} fusion(bf16[512,1792]{1,0:T(8,128)(2,1)S(1)} %copy-done, bf16[1024,1792]{1,0:T(8,128)(2,1)} %all-gather.6.cloned.1.call-done, s32[1024]{0:T(1024)S(1)} %add_select_fusion, s32[512]{0:T(512)S(1)} %bitcast.52), kind=kOutput, calls=%fused_computation.17 | convolution fusion | flops 1880096768 | bytes 7608320 | tf_op jit(solution)/shard_map/dot_general | solution.py:240
  63.4 0.5 copy.32
  63.8 0.6 bitcast_reduce_fusion
  64.4 0.1 copy.23
  64.5 43.9 %all-gather.4.cloned.1.call-done = bf16[1024,1792]{1,0:T(8,128)(2,1)} async-done(((bf16[64,1792]{1,0:T(8,128)(2,1)}), bf16[1024,1792]{1,0:T(8,128)(2,1)}) %all-gather.4.cloned.1.call-update) | async-done | bytes 3670032 | tf_op jit(solution)/shard_map/all_gather | solution.py:246
  108.5 4.7 %fusion.14 = f32[64,8,8,128]{3,1,2,0:T(8,128)S(1)} fusion(bf16[512,1792]{1,0:T(8,128)(2,1)} %param.7, bf16[1024,1792]{1,0:T(8,128)(2,1)} %all-gather.4.cloned.1.call-done, s32[1024]{0:T(1024)S(1)} %add_select_fusion, s32[512]{0:T(512)S(1)} %bitcast.53), kind=kOutput, calls=%fused_computation.16 | convolution fusion | flops 1880096768 | bytes 7608320 | tf_op jit(solution)/shard_map/dot_general | solution.py:240
  113.1 0.5 copy.31
  113.6 0.6 bitcast_reduce_fusion.1
  114.2 0.1 copy.22
  114.4 1.5 collective-permute-start.1
  115.9 7.5 %fusion.11 = bf16[512,1792]{0,1:T(8,128)(2,1)} fusion(bf16[512,1792]{1,0:T(8,128)(2,1)S(1)} %copy-done, bf16[3584,1792]{1,0:T(8,128)(2,1)} %param.9, s32[]{:T(128)S(6)} %select_n.34), kind=kOutput, calls=%fused_computation.15 | convolution fusion | flops 3289251840 | bytes 10092548 | tf_op jit(solution)/shard_map/dot_general | solution.py:240
  123.4 0.6 collective-permute-start
  124.0 0.0 collective-permute-done.1
  124.0 0.1 tile.8
  124.1 1.3 copy.24
  125.5 0.1 tile.20
  125.6 1.3 copy.26
  126.9 0.0 copy-start.1
  126.9 5.9 %multiply_convert_fusion.1 = bf16[1024,1792]{1,0:T(8,128)(2,1)} fusion(bf16[512,1792]{1,0:T(8,128)(2,1)} %param.7, bf16[512,1024]{1,0:T(8,128)(2,1)} %copy.24, s32[1024]{0:T(1024)S(1)} %add_select_fusion, s32[512]{0:T(512)S(1)} %bitcast.54), kind=kOutput, calls=%fused_computation.1 | convolution fusion | flops 1883766784 | bytes 6559744 | tf_op jit(solution)/shard_map/dot_general | solution.py:240
  132.9 0.0 copy-done.1
  132.9 4.1 %multiply_convert_fusion = bf16[1024,1792]{1,0:T(8,128)(2,1)} fusion(bf16[512,1792]{1,0:T(8,128)(2,1)S(1)} %copy-done, bf16[512,1024]{1,0:T(8,128)(2,1)S(1)} %copy-done.1, s32[1024]{0:T(1024)S(1)} %add_select_fusion, s32[512]{0:T(512)S(1)} %bitcast.55), kind=kOutput, calls=%fused_computation | convolution fusion | flops 1883766784 | bytes 6559744 | tf_op jit(solution)/shard_map/dot_general | solution.py:240
  137.0 66.9 %shard_map.110 = f32[2,64,1792]{2,1,0:T(8,128)} custom-call(bf16[4,2,2,64,1792]{4,3,2,1,0:T(8,128)(2,1)} %bitcast.46, bf16[4,2,2,64,1792]{4,3,2,1,0:T(8,128)(2,1)} %bitcast.47), custom_call_target="tpu_custom_call" | custom-call | flops 7340032 | bytes 73400320 | tf_op jit(solution)/shard_map/pallas_call | solution.py:210
  203.9 1.2 fusion.29
  205.1 0.2 multiply_reduce_fusion
  205.3 0.2 dynamic-update-slice
  205.5 38.3 %all-reduce = f32[128]{0:T(128)S(1)} all-reduce(f32[128]{0:T(128)S(1)} %dynamic-update-slice), channel_id=2, replica_groups=mesh['aa'=16,'ba'=2] {'aa','ba'}, use_global_device_ids=true, to_apply=%add | all-reduce | flops 128 | bytes 1024
  243.8 0.1 reshape.63
  243.9 0.6 reduce_sum.69
  244.5 4.6 %multiply_convert_fusion.2 = bf16[512,1792]{0,1:T(8,128)(2,1)S(1)} fusion(bf16[1024,1792]{1,0:T(8,128)(2,1)} %all-gather.4.cloned.1.call-done, bf16[512,1024]{1,0:T(8,128)(2,1)} %copy.24, s32[1024]{0:T(1024)S(1)} %add_select_fusion, s32[512]{0:T(512)S(1)} %bitcast.56), kind=kOutput, calls=%fused_computation.13 | convolution fusion | flops 1881931776 | bytes 6559744 | tf_op jit(solution)/shard_map/dot_general | solution.py:240
  249.1 0.0 collective-permute-done
  249.1 7.9 %fusion.5 = bf16[512,1792]{0,1:T(8,128)(2,1)} fusion(bf16[512,1792]{0,1:T(8,128)(2,1)S(1)} %multiply_convert_fusion.2, bf16[512,1792]{0,1:T(8,128)(2,1)} %collective-permute-done, bf16[512,1792]{1,0:T(8,128)(2,1)S(1)} %copy-done, bf16[3584,1792]{1,0:T(8,128)(2,1)} %param.9, s32[]{:T(128)S(6)} %select_n.33), kind=kOutput, calls=%fused_computation.12 | convolution fusion | flops 3292921856 | bytes 13762564 | tf_op jit(solution)/shard_map/dot_general | solution.py:240
  257.0 3.8 %copy.29 = bf16[512,1792]{1,0:T(8,128)(2,1)} copy(bf16[512,1792]{0,1:T(8,128)(2,1)} %fusion.5) | data formatting | bytes 3670016
  261.6 3.7 %multiply_subtract_fusion = (f32[4,2,16,1792]{3,2,1,0:T(8,128)}, f32[4,2,16,1792]{3,2,1,0:T(8,128)}, f32[4,2,16,1792]{3,2,1,0:T(8,128)}) fusion(f32[4,2,16,1792]{3,2,1,0:T(8,128)} %param.11, f32[4]{0:T(128)S(1)} %maximum_divide_fusion, f32[4,1,16,1792]{3,2,1,0:T(8,128)S(1)} %bitcast.45, f32[4,1,16,1792]{3,2,1,0:T(8,128)S(1)} %bitcast.43, ...), kind=kLoop, calls=%fused_computation.25 | loop fusion | flops 3211264 | bytes 6422544 | tf_op jit(solution)/shard_map/sub | solution.py:31
  (9 shorter events, 0.1 us)
Async XLA Ops:
  7.2 52.1 %copy-start = (bf16[512,1792]{1,0:T(8,128)(2,1)S(1)}, bf16[512,1792]{1,0:T(8,128)(2,1)}, u32[]{:S(2)}) copy-start(bf16[512,1792]{1,0:T(8,128)(2,1)} %param.8) | copy-start | bytes 5505028
  7.2 52.0 %copy-start.2 = (s32[512,1]{0,1:T(1,128)S(1)}, s32[512,1]{0,1:T(1,128)}, u32[]{:S(2)}) copy-start(s32[512,1]{0,1:T(1,128)} %param.10) | copy-start | bytes 6148
  7.2 52.0 %all-gather.6.cloned.1.call-start = ((), (), s32[]{:S(2)}) async-start(), calls=%async_computation.1 | async-start | bytes 3899392 | tf_op jit(solution)/shard_map/all_gather | solution.py:245
  9.4 99.0 %all-gather.4.cloned.1.call-start = ((), (), s32[]{:S(2)}) async-start(), calls=%async_computation | async-start | bytes 3899392 | tf_op jit(solution)/shard_map/all_gather | solution.py:246
  114.4 9.6 %collective-permute-start.1 = (f32[512,32]{0,1:T(8,128)S(1)}, f32[512,32]{0,1:T(8,128)S(1)}, u32[]{:S(2)}, u32[]{:S(2)}) collective-permute-start(f32[512,32]{0,1:T(8,128)S(1)} %pad_maximum_fusion.1), channel_id=1, source_target_pairs={{0,1},{1,0},{2,3},{3,2},{4,5},{5,4},{6,7},{7,6},{8,9},{9,8},{10,11... | collective-permute-start | bytes 196616 | tf_op jit(solution)/shard_map/ppermute | solution.py:253
  123.4 125.7 %collective-permute-start = (bf16[512,1792]{0,1:T(8,128)(2,1)}, bf16[512,1792]{0,1:T(8,128)(2,1)}, u32[]{:S(2)}, u32[]{:S(2)}) collective-permute-start(bf16[512,1792]{0,1:T(8,128)(2,1)} %fusion.11), channel_id=1, source_target_pairs={{0,1},{1,0},{2,3},{3,2},{4,5},{5,4},{6,7},{7,6},{8,9},{9,8},{10,11... | collective-permute-start | bytes 5505032 | tf_op jit(solution)/shard_map/ppermute | solution.py:251
  126.9 6.0 %copy-start.1 = (bf16[512,1024]{1,0:T(8,128)(2,1)S(1)}, bf16[512,1024]{1,0:T(8,128)(2,1)}, u32[]{:S(2)}) copy-start(bf16[512,1024]{1,0:T(8,128)(2,1)} %copy.26) | copy-start | bytes 3145732
Sparse Core Ops, SparseCore 0:
  10.9 48.3 all-gather.5
  62.1 46.3 all-gather.3

commit v2 on v1

--- a/solution.py
+++ b/solution.py
@@ -248,16 +248,18 @@
         swap = [(0, 1), (1, 0)]
         rows_of = lambda k: lax.dynamic_slice_in_dim(base_weight, k * width, width, axis=0)
         away = dot(cotangent, rows_of(1 - side), ((1,), (1,))).astype(jnp.bfloat16)
+        cot_away, away = lax.optimization_barrier((cotangent, away))
         away = lax.ppermute(away, "ba", swap)
-        frozen_term = dot(cotangent, rows_of(side), ((1,), (1,)))
+        frozen_term = dot(cot_away, rows_of(side), ((1,), (1,)))
         both = lambda a: a + lax.ppermute(a, "ba", swap)
     else:
         partial_sums = dot(cotangent, base_weight, ((1,), (1,)))
         frozen_term = lax.psum_scatter(partial_sums, "ba", scatter_dimension=1, tiled=True)
         away = jnp.zeros((), jnp.bfloat16)
         both = lambda a: lax.psum(a, "ba")
+    cot_after, frozen_term = lax.optimization_barrier((cotangent, frozen_term))
     mine = adapter_ids == (jnp.arange(total * rank, dtype=jnp.int32) // rank)[None, :]
-    pulled = jnp.where(mine, dot(cotangent, up, ((1,), (1,))), 0.0)
+    pulled = jnp.where(mine, dot(cot_after, up, ((1,), (1,))), 0.0)
     projected = jnp.where(mine, dot(inputs, down, ((1,), (1,))), 0.0)
     fold = lambda a: a.reshape(tok_rows, total * rank // 128, 128).sum(axis=1)
     fold2 = lambda a: fold(a).reshape(tok_rows, 128 // rank, rank).sum(axis=1)
@@ -277,12 +279,20 @@
         [summed[k].reshape(local_count, rank, width) for k in range(2)], axis=1
     )
     part_squares = jnp.sum(gradients * gradients, axis=(1, 2, 3))
-    every = lax.all_gather(part_squares, ("aa", "ba")).reshape(owners, halves, local_count)
-    squares = lax.dynamic_index_in_dim(every, lax.axis_index("aa"), 0, False).sum(axis=0)
+    squares = both(part_squares)
+    grand_total = jnp.sum(squares)
+    if owners & (owners - 1) == 0:
+        stride = 1
+        while stride < owners:
+            pairs = [(k, k ^ stride) for k in range(owners)]
+            grand_total = grand_total + lax.ppermute(grand_total, "aa", pairs)
+            stride *= 2
+    else:
+        grand_total = lax.psum(grand_total, "aa")
     new_adapters, new_first, new_second = adam_update(
         adapters, first_moment, second_moment, gradients, squares
     )
-    return (input_gradient, new_adapters, new_first, new_second, jnp.sqrt(jnp.sum(every)))
+    return (input_gradient, new_adapters, new_first, new_second, jnp.sqrt(grand_total))
 
 
 def solution(mesh):

time: 277 us -> 246 us (0.89)
  blocking collectives: 38.3 us -> 0 us
  waiting for transfers between devices: 93.7 us -> 84 us
  starting transfers between devices: 2.17 us -> 10.7 us
  local copies, waits for them, and re-layouts: 10.3 us -> 15.3 us
  between operations: 16 us -> 18.8 us
    unnamed x1 -> x0, blocking collectives: 38.3 us -> none
    all_gather x1, waiting for transfers between devices: 49 us -> 31.6 us  [local(): up = lax.all_gather(own(1), 'aa', axis=0, tiled=True)]
    ppermute x0 -> x4, starting transfers between devices: none -> 6.99 us  [local(): grand_total = grand_total + lax.ppermute(grand_total, 'aa', pairs)]
    optimization_barrier x0 -> x1, local copies, waits for them, and re-layouts: none -> 5.13 us  [local(): cot_after, frozen_term = lax.optimization_barrier((cotangent, frozen_term))]
    ppermute x0 -> x4, waiting for transfers between devices: none -> 4.67 us  [local(): grand_total = grand_total + lax.ppermute(grand_total, 'aa', pairs)]
    ppermute x1 -> x2, waiting for transfers between devices: 0.01 us -> 3.02 us  [local(): both = lambda a: a + lax.ppermute(a, 'ba', swap)]
  transfers between devices with their start and end apart: 4 -> 9, of which waited for: 2 -> 6; matrix products, arithmetic and copies ran while one was open for 12% -> 17% of each run, Pallas kernels for 24% -> 0%
where the time goes in v2:
time: 246 us; the launch traced here: 243 us
  waiting for transfers between devices  84 us (34%)
  Pallas kernels  67.5 us (27%)
  matrix products  41.4 us (17%)
  between operations  18.8 us (8%)
  local copies, waits for them, and re-layouts  15.3 us (6%)
  starting transfers between devices  10.7 us (4%)
  other arithmetic  5.31 us (2%)
    pallas_call x1, Pallas kernels, reduce_scatter(): pl.pallas_call(functools.partial(scatter_kernel, outer, inner), out_shape...  67.5 us
    all_gather x1, waiting for transfers between devices, local(): down = lax.all_gather(own(0), 'aa', axis=0, tiled=True)  43.9 us
    dot_general x7, matrix products, local(): lax.dot_general(a, b, (dims, ((), ())), preferred_element_type=jnp.float32)  41.4 us
    all_gather x1, waiting for transfers between devices, local(): up = lax.all_gather(own(1), 'aa', axis=0, tiled=True)  31.6 us
    ppermute x4, starting transfers between devices, local(): grand_total = grand_total + lax.ppermute(grand_total, 'aa', pairs)  6.99 us
    optimization_barrier x1, local copies, waits for them, and re-layouts, local(): cot_after, frozen_term = lax.optimization_barrier((cotangent, frozen_term))  5.13 us
  transfers between devices with their start and end apart: 9, of which 6 were waited for; matrix products, arithmetic and copies ran while one was open for 17% of the time, Pallas kernels for 0%

profile of v2, /device:TPU:16, one launch (start us, length us, event | category | flops | bytes accessed | tf_op | source)
XLA Modules:
  0.0 242.9 jit_solution(13623153216204801104)
XLA Ops:
  7.2 0.0 copy-start
  7.2 0.0 all-gather.5.cloned.1.call-start
  7.2 1.4 convert_element_type.33
  8.6 0.8 fusion.26
  9.4 0.0 all-gather.5.cloned.1.call-update
  9.4 0.0 all-gather.3.cloned.1.call-start
  9.5 0.7 all-gather.3.cloned.1.call-update
  10.2 0.0 copy-done
  10.2 7.5 %fusion.7 = bf16[512,1792]{0,1:T(8,128)(2,1)} fusion(bf16[512,1792]{1,0:T(8,128)(2,1)S(1)} %copy-done, bf16[3584,1792]{1,0:T(8,128)(2,1)} %param.9, s32[]{:T(128)S(6)} %select_n.29), kind=kOutput, calls=%fused_computation.13 | convolution fusion | flops 3289251840 | bytes 10092548 | tf_op jit(solution)/shard_map/dot_general | solution.py:240
  17.7 1.5 collective-permute-start
  19.2 0.0 copy-start.7
  19.2 8.4 %fusion = f32[512,1792]{1,0:T(8,128)} fusion(bf16[512,1792]{1,0:T(8,128)(2,1)S(1)} %copy-done, bf16[3584,1792]{1,0:T(8,128)(2,1)} %param.9, s32[]{:T(128)S(6)} %select_n.30), kind=kOutput, calls=%fused_computation.2 | convolution fusion | flops 3288334336 | bytes 11927556 | tf_op jit(solution)/shard_map/dot_general | solution.py:240
  27.6 31.6 %all-gather.5.cloned.1.call-done = bf16[1024,1792]{1,0:T(8,128)(2,1)} async-done(((bf16[64,1792]{1,0:T(8,128)(2,1)}), bf16[1024,1792]{1,0:T(8,128)(2,1)}) %all-gather.5.cloned.1.call-update) | async-done | bytes 3670032 | tf_op jit(solution)/shard_map/all_gather | solution.py:245
  59.2 0.0 copy-done.7
  59.2 4.1 %fusion.11 = f32[64,8,8,128]{3,1,2,0:T(8,128)S(1)} fusion(bf16[512,1792]{1,0:T(8,128)(2,1)S(1)} %copy-done, bf16[1024,1792]{1,0:T(8,128)(2,1)} %all-gather.5.cloned.1.call-done, s32[1024]{0:T(1024)S(1)} %add_select_fusion, s32[512]{0:T(512)S(1)} %bitcast.46), kind=kOutput, calls=%fused_computation.15 | convolution fusion | flops 1880096768 | bytes 7608320 | tf_op jit(solution)/shard_map/dot_general | solution.py:240
  63.3 0.5 copy.35
  63.8 0.6 bitcast_reduce_fusion
  64.4 0.1 copy.26
  64.5 43.9 %all-gather.3.cloned.1.call-done = bf16[1024,1792]{1,0:T(8,128)(2,1)} async-done(((bf16[64,1792]{1,0:T(8,128)(2,1)}), bf16[1024,1792]{1,0:T(8,128)(2,1)}) %all-gather.3.cloned.1.call-update) | async-done | bytes 3670032 | tf_op jit(solution)/shard_map/all_gather | solution.py:246
  108.4 4.7 %fusion.10 = f32[64,8,8,128]{3,1,2,0:T(8,128)S(1)} fusion(bf16[512,1792]{1,0:T(8,128)(2,1)} %param.7, bf16[1024,1792]{1,0:T(8,128)(2,1)} %all-gather.3.cloned.1.call-done, s32[1024]{0:T(1024)S(1)} %add_select_fusion, s32[512]{0:T(512)S(1)} %bitcast.47), kind=kOutput, calls=%fused_computation.14 | convolution fusion | flops 1880096768 | bytes 7608320 | tf_op jit(solution)/shard_map/dot_general | solution.py:240
  113.1 0.5 copy.34
  113.6 0.6 bitcast_reduce_fusion.1
  114.2 0.1 copy.25
  114.4 1.5 collective-permute-start.1
  115.9 5.1 %copy.24 = f32[512,1792]{0,1:T(8,128)} copy(f32[512,1792]{1,0:T(8,128)} %fusion) | data formatting | bytes 7340032 | tf_op jit(solution)/shard_map/optimization_barrier | solution.py:260
  121.0 0.0 collective-permute-done.1
  121.1 0.1 tile.8
  121.2 1.3 copy.27
  122.5 0.0 copy-start.1
  122.5 0.0 copy-start.3
  122.5 0.0 copy-start.6
  122.5 6.0 %multiply_convert_fusion.1 = bf16[1024,1792]{1,0:T(8,128)(2,1)} fusion(bf16[512,1792]{1,0:T(8,128)(2,1)} %param.7, bf16[512,1024]{1,0:T(8,128)(2,1)} %copy.27, s32[1024]{0:T(1024)S(1)} %add_select_fusion, s32[512]{0:T(512)S(1)} %bitcast.48), kind=kOutput, calls=%fused_computation.1 | convolution fusion | flops 1883766784 | bytes 6559744 | tf_op jit(solution)/shard_map/dot_general | solution.py:240
  128.5 0.0 collective-permute-done
  128.5 0.0 copy-done.1
  128.5 0.0 copy-done.3
  128.5 0.0 copy-done.6
  128.5 5.5 %add_convert_fusion = bf16[512,1792]{0,1:T(8,128)(2,1)} fusion(f32[512,1792]{0,1:T(8,128)S(1)} %copy-done.1, bf16[512,1792]{0,1:T(8,128)(2,1)} %collective-permute-done, bf16[1024,1792]{1,0:T(8,128)(2,1)S(1)} %copy-done.6, bf16[512,1024]{1,0:T(8,128)(2,1)S(1)} %copy-done.3, s32[1024]{0:T(1024)S(1)} %add_select_fusion, s32[512]{0:T(512)S(1)} %bitcast.49), kind=kOutput, calls=%fused_computation.10 | convolution fusion | flops 1886519296 | bytes 12064768 | tf_op jit(solution)/shard_map/dot_general | solution.py:240
  134.0 3.8 %copy.32 = bf16[512,1792]{1,0:T(8,128)(2,1)} copy(bf16[512,1792]{0,1:T(8,128)(2,1)} %add_convert_fusion) | data formatting | bytes 3670016
  137.8 0.1 tile.20
  137.9 1.4 copy.29
  139.3 5.2 %multiply_convert_fusion = bf16[1024,1792]{1,0:T(8,128)(2,1)} fusion(bf16[512,1792]{1,0:T(8,128)(2,1)S(1)} %copy-done, bf16[512,1024]{1,0:T(8,128)(2,1)} %copy.29, s32[1024]{0:T(1024)S(1)} %add_select_fusion, s32[512]{0:T(512)S(1)} %bitcast.50), kind=kOutput, calls=%fused_computation | convolution fusion | flops 1883766784 | bytes 6559744 | tf_op jit(solution)/shard_map/dot_general | solution.py:240
  144.5 67.5 %shard_map.110 = f32[2,64,1792]{2,1,0:T(8,128)} custom-call(bf16[4,2,2,64,1792]{4,3,2,1,0:T(8,128)(2,1)} %bitcast.40, bf16[4,2,2,64,1792]{4,3,2,1,0:T(8,128)(2,1)} %bitcast.41), custom_call_target="tpu_custom_call" | custom-call | flops 7340032 | bytes 73400320 | tf_op jit(solution)/shard_map/pallas_call | solution.py:210
  212.0 0.0 copy-start.2
  212.1 0.0 copy-start.4
  212.1 0.0 copy-start.5
  212.1 1.4 fusion.25
  213.4 0.2 multiply_reduce_fusion
  213.6 0.6 collective-permute-start.2
  214.2 3.0 %collective-permute-done.2 = f32[4]{0:T(128)S(1)} collective-permute-done((f32[4]{0:T(128)S(1)}, f32[4]{0:T(128)S(1)}, u32[]{:S(2)}, u32[]{:S(2)}) %collective-permute-start.2) | collective-permute-done | bytes 48 | tf_op jit(solution)/shard_map/ppermute | solution.py:254
  217.2 0.6 add_reduce_fusion
  217.8 0.0 collective-permute-start.3
  217.8 0.0 copy-done.2
  217.8 0.0 copy-done.4
  217.9 0.0 copy-done.5
  217.9 2.0 multiply_subtract_fusion
  219.9 0.0 collective-permute-done.3
  221.2 2.3 collective-permute-start.4
  223.5 1.3 collective-permute-done.4
  225.5 2.0 collective-permute-start.5
  227.5 1.6 collective-permute-done.5
  229.7 2.7 %collective-permute-start.6 = (f32[]{:T(128)}, f32[]{:T(128)}, u32[]{:S(2)}, u32[]{:S(2)}) collective-permute-start(f32[]{:T(128)} %add.59), channel_id=1, source_target_pairs={{0,16},{2,18},{4,20},{6,22},{8,24},{10,26},{12,28},{14,30},{16,0},... | collective-permute-start | bytes 20 | tf_op jit(solution)/shard_map/ppermute | solution.py:288
  232.4 1.8 collective-permute-done.6
  (6 shorter events, 0.1 us)
Async XLA Ops:
  7.2 3.0 %copy-start = (bf16[512,1792]{1,0:T(8,128)(2,1)S(1)}, bf16[512,1792]{1,0:T(8,128)(2,1)}, u32[]{:S(2)}) copy-start(bf16[512,1792]{1,0:T(8,128)(2,1)} %param.8) | copy-start | bytes 5505028
  7.2 52.0 %all-gather.5.cloned.1.call-start = ((), (), s32[]{:S(2)}) async-start(), calls=%async_computation.1 | async-start | bytes 3899392 | tf_op jit(solution)/shard_map/all_gather | solution.py:245
  9.4 99.0 %all-gather.3.cloned.1.call-start = ((), (), s32[]{:S(2)}) async-start(), calls=%async_computation | async-start | bytes 3899392 | tf_op jit(solution)/shard_map/all_gather | solution.py:246
  17.7 110.8 %collective-permute-start = (bf16[512,1792]{0,1:T(8,128)(2,1)}, bf16[512,1792]{0,1:T(8,128)(2,1)}, u32[]{:S(2)}, u32[]{:S(2)}) collective-permute-start(bf16[512,1792]{0,1:T(8,128)(2,1)} %fusion.7), channel_id=1, source_target_pairs={{0,1},{1,0},{2,3},{3,2},{4,5},{5,4},{6,7},{7,6},{8,9},{9,8},{10,11... | collective-permute-start | bytes 5505032 | tf_op jit(solution)/shard_map/ppermute | solution.py:252
  19.2 40.0 %copy-start.7 = (s32[512,1]{0,1:T(1,128)S(1)}, s32[512,1]{0,1:T(1,128)}, u32[]{:S(2)}) copy-start(s32[512,1]{0,1:T(1,128)} %param.10) | copy-start | bytes 6148
  114.4 6.7 %collective-permute-start.1 = (f32[512,32]{0,1:T(8,128)S(1)}, f32[512,32]{0,1:T(8,128)S(1)}, u32[]{:S(2)}, u32[]{:S(2)}) collective-permute-start(f32[512,32]{0,1:T(8,128)S(1)} %pad_maximum_fusion.1), channel_id=1, source_target_pairs={{0,1},{1,0},{2,3},{3,2},{4,5},{5,4},{6,7},{7,6},{8,9},{9,8},{10,11... | collective-permute-start | bytes 196616 | tf_op jit(solution)/shard_map/ppermute | solution.py:254
  122.5 6.0 %copy-start.1 = (f32[512,1792]{0,1:T(8,128)S(1)}, f32[512,1792]{0,1:T(8,128)}, u32[]{:S(2)}) copy-start(f32[512,1792]{0,1:T(8,128)} %copy.24) | copy-start | bytes 11010052
  122.5 6.0 %copy-start.3 = (bf16[512,1024]{1,0:T(8,128)(2,1)S(1)}, bf16[512,1024]{1,0:T(8,128)(2,1)}, u32[]{:S(2)}) copy-start(bf16[512,1024]{1,0:T(8,128)(2,1)} %copy.27) | copy-start | bytes 3145732
  122.5 6.0 %copy-start.6 = (bf16[1024,1792]{1,0:T(8,128)(2,1)S(1)}, bf16[1024,1792]{1,0:T(8,128)(2,1)}, u32[]{:S(2)}) copy-start(bf16[1024,1792]{1,0:T(8,128)(2,1)} %all-gather.3.cloned.1.call-done) | copy-start | bytes 11010052
  212.0 5.8 %copy-start.2 = (f32[4,2,16,1792]{3,2,1,0:T(8,128)S(1)}, f32[4,2,16,1792]{3,2,1,0:T(8,128)}, u32[]{:S(2)}) copy-start(f32[4,2,16,1792]{3,2,1,0:T(8,128)} %param.11) | copy-start | bytes 2752516
  212.1 5.8 %copy-start.4 = (f32[4,2,16,1792]{3,2,1,0:T(8,128)S(1)}, f32[4,2,16,1792]{3,2,1,0:T(8,128)}, u32[]{:S(2)}) copy-start(f32[4,2,16,1792]{3,2,1,0:T(8,128)} %param.13) | copy-start | bytes 2752516
  212.1 5.8 %copy-start.5 = (f32[4,2,16,1792]{3,2,1,0:T(8,128)S(1)}, f32[4,2,16,1792]{3,2,1,0:T(8,128)}, u32[]{:S(2)}) copy-start(f32[4,2,16,1792]{3,2,1,0:T(8,128)} %param.12) | copy-start | bytes 2752516
  213.6 3.6 %collective-permute-start.2 = (f32[4]{0:T(128)S(1)}, f32[4]{0:T(128)S(1)}, u32[]{:S(2)}, u32[]{:S(2)}) collective-permute-start(f32[4]{0:T(128)S(1)} %multiply_reduce_fusion), channel_id=1, source_target_pairs={{0,1},{1,0},{2,3},{3,2},{4,5},{5,4},{6,7},{7,6},{8,9},{9,8},{10,11... | collective-permute-start | bytes 56 | tf_op jit(solution)/shard_map/ppermute | solution.py:254
  217.8 2.0 collective-permute-start.3
  221.2 3.6 %collective-permute-start.4 = (f32[]{:T(128)}, f32[]{:T(128)}, u32[]{:S(2)}, u32[]{:S(2)}) collective-permute-start(f32[]{:T(128)} %add.57), channel_id=1, source_target_pairs={{0,4},{2,6},{4,0},{6,2},{8,12},{10,14},{12,8},{14,10},{16,20},{18,... | collective-permute-start | bytes 20 | tf_op jit(solution)/shard_map/ppermute | solution.py:288
  225.5 3.6 %collective-permute-start.5 = (f32[]{:T(128)}, f32[]{:T(128)}, u32[]{:S(2)}, u32[]{:S(2)}) collective-permute-start(f32[]{:T(128)} %add.58), channel_id=1, source_target_pairs={{0,8},{2,10},{4,12},{6,14},{8,0},{10,2},{12,4},{14,6},{16,24},{18,... | collective-permute-start | bytes 20 | tf_op jit(solution)/shard_map/ppermute | solution.py:288
  229.7 4.5 %collective-permute-start.6 = (f32[]{:T(128)}, f32[]{:T(128)}, u32[]{:S(2)}, u32[]{:S(2)}) collective-permute-start(f32[]{:T(128)} %add.59), channel_id=1, source_target_pairs={{0,16},{2,18},{4,20},{6,22},{8,24},{10,26},{12,28},{14,30},{16,0},... | collective-permute-start | bytes 20 | tf_op jit(solution)/shard_map/ppermute | solution.py:288
Sparse Core Ops, SparseCore 0:
  10.8 48.3 all-gather.4
  62.1 46.3 all-gather.2
